TPU v7x, 128 devices: a whole 4x4x4 slice. The times are simulated.
128 devices in a mesh: prompt: 16 (over z, x_lo, core), ctx: 8 (over x_hi, y).
Axes of the slice: x: 4 (x_hi: 2, x_lo: 2; x = x_hi * 2 + x_lo), y: 4, z: 4, core: 2. Of those that a mesh axis runs over, the one named last changes fastest.
Arguments:
- queries: bfloat16 [65536, 16, 128], P(('prompt', 'ctx')), may hold values from -8 to 8
- keys: bfloat16 [65536, 4, 128], P(('prompt', 'ctx')), may hold values from -8 to 8
- values: bfloat16 [65536, 4, 128], P(('prompt', 'ctx')), may hold values from -6 to 6
- spans: int32 [16, 2], P('prompt'), may hold values from 1 to 3072, as said below
- partner: int32 [16], replicated, may hold values from 0 to 15, each once
Outputs:
- attended: bfloat16 [65536, 16, 128], P(('prompt', 'ctx'))
- decode_cache: bfloat16 [16, 2, 16, 8, 128, 128], P('ctx', None, 'prompt')
Inputs may be any that keep to these rules, and one draw needn't show every extreme that they name: `spans`: column 0 counts the image tokens of a prompt, from 1024 to 2048, which come first; column 1 counts the text tokens after them, 1 or more; the two sum to at most 4096, and to exactly 4096 for at least one prompt.
All inputs are finite; a program needn't handle non-finite values.
Results may differ from a plain program's by a relative error of at most 0.0041.
Values may be sent and summed in bfloat16 or wider, within the bound.
A program may use at most 64 MiB of HBM per device.

v0:
```python
import functools
import math

import jax
import jax.numpy as jnp
from jax import lax
from jax.experimental import pallas as pl
from jax.experimental.pallas import tpu as pltpu
from jax.sharding import PartitionSpec as P

LOG2E = 1.4426950408889634
MESH = pl.DeviceIdType.MESH
ROUNDS = 10
CROSS = 8
DOT = (((1,), (0,)), ((), ()))


def fused_kernel(
    len_ref, partner_ref, q_ref, k_ref, v_ref, o_ref, cache_ref,
    own, inbox, relay, qt, peak, acc, score_a, score_b, spread, gathered, chosen, wide,
    link_send, link_recv, relay_recv, spread_send, spread_recv, hand_send, hand_recv,
):
    heads, rows, width = q_ref.shape
    groups = k_ref.shape[0]
    members = heads // groups
    tiles = rows // width
    scale = LOG2E / math.sqrt(width)
    scores = (score_a, score_b)

    prompts, blocks = lax.axis_size("prompt"), lax.axis_size("ctx")
    p, c = lax.axis_index("prompt"), lax.axis_index("ctx")
    ring = blocks // 2
    half, y = c // ring, c % ring
    flipped = p + 2 - 4 * ((p // 2) % 2)
    ahead = (p, half * ring + (y + 1) % ring)
    behind = (p, half * ring + (y + ring - 1) % ring)
    beside = (flipped, c)
    across = (flipped, (1 - half) * ring + y)
    length = len_ref[0]

    barrier = pltpu.get_barrier_semaphore()

    def greet_prompt(k, carry):
        pl.semaphore_signal(barrier, inc=1, device_id=((p + k) % prompts, c), device_id_type=MESH)
        return carry

    def greet_ctx(k, carry):
        pl.semaphore_signal(barrier, inc=1, device_id=(p, (c + k) % blocks), device_id_type=MESH)
        return carry

    lax.fori_loop(1, prompts, greet_prompt, 0)
    lax.fori_loop(1, blocks, greet_ctx, 0)
    pl.semaphore_signal(barrier, inc=1, device_id=across, device_id_type=MESH)

    for g in range(groups):
        own[g, 0:rows, :] = k_ref[g]
        for t in range(tiles):
            own[g, rows + t * width : rows + (t + 1) * width, :] = v_ref[
                g, t * width : (t + 1) * width, :
            ].T
    pl.semaphore_wait(barrier, prompts + blocks - 1)

    def put(src, dst, lane, i, recv, target):
        return pltpu.make_async_remote_copy(
            src_ref=src, dst_ref=dst, send_sem=link_send.at[lane, i], recv_sem=recv,
            device_id=target, device_id_type=MESH,
        )

    def send_ahead(i):
        @pl.when(i < 4)
        def _():
            put(own.at[i], inbox.at[0, i], 0, i, link_recv.at[0, i], ahead).start()

        @pl.when((i >= 4) & (i < 8))
        def _():
            put(inbox.at[0, i - 4], inbox.at[0, i], 0, i, link_recv.at[0, i], ahead).start()

        @pl.when((i >= 8) & (i < ROUNDS))
        def _():
            put(inbox.at[2, i - 3], inbox.at[0, i], 0, i, link_recv.at[0, i], ahead).start()

    def send_behind(i):
        @pl.when(i < 4)
        def _():
            put(own.at[i], inbox.at[1, i], 1, i, link_recv.at[1, i], behind).start()

        @pl.when((i >= 4) & (i < 8))
        def _():
            put(inbox.at[2, i - 3], inbox.at[1, i], 1, i, link_recv.at[1, i], behind).start()

        @pl.when((i >= 8) & (i < ROUNDS))
        def _():
            put(inbox.at[1, i - 4], inbox.at[1, i], 1, i, link_recv.at[1, i], behind).start()

    def send_beside(i):
        @pl.when(i < 4)
        def _():
            put(own.at[i], relay.at[i], 2, i, relay_recv.at[i], beside).start()

        @pl.when((i >= 4) & (i < CROSS))
        def _():
            put(inbox.at[0, (i - 2) % 4], relay.at[i], 2, i, relay_recv.at[i], beside).start()

    def send_across(i):
        put(relay.at[i], inbox.at[2, i + 1], 3, i, link_recv.at[2, i + 1], across).start()

    for i in range(2):
        send_ahead(jnp.int32(i))
        send_behind(jnp.int32(i))
        send_beside(jnp.int32(i))

    position = c * rows + lax.broadcasted_iota(jnp.int32, (rows, width), 0)
    stripes = spread.shape[0] // groups
    stripe_rows = rows // stripes
    for part, ref in enumerate((k_ref, v_ref)):
        for g in range(groups):
            wide[...] = jnp.where(position < length, ref[g].astype(jnp.float32), 0.0)
            for st in range(stripes):
                spread[st * groups + g, part] = wide[pl.ds(st, stripe_rows, stride=stripes), :].astype(jnp.bfloat16)

    def spread_copy(s):
        return pltpu.make_async_remote_copy(
            src_ref=spread.at[s], dst_ref=gathered.at[p], send_sem=spread_send.at[s],
            recv_sem=spread_recv.at[p], device_id=(s, c), device_id_type=MESH,
        )

    def spread_start(k, carry):
        spread_copy((p + k) % prompts).start()
        return carry

    gathered[p] = spread[p]
    lax.fori_loop(1, prompts, spread_start, 0)

    def turn(n, carry):
        qt[n] = q_ref[n].T
        peak[n] = jnp.full((1, rows), -1e30, jnp.float32)
        acc[n] = jnp.zeros(acc.shape[1:], jnp.float32)
        return carry

    lax.fori_loop(0, heads, turn, 0)

    def score(chunk, g, m):
        return lax.dot_general(
            chunk[0:rows, :], qt[g * members + m], DOT, preferred_element_type=jnp.float32
        )

    def fold(chunk, g, m, s, mask):
        n = g * members + m
        if mask is not None:
            s = jnp.where(mask, s, -1e30)
        before = peak[n]
        top = jnp.maximum(before, jnp.max(s, axis=0, keepdims=True))
        weight = jnp.exp2(s * scale - top * scale).astype(jnp.bfloat16)
        turned = jnp.concatenate(
            [chunk[rows + t * width : rows + (t + 1) * width, :] for t in range(tiles)], axis=1
        )
        turned = jnp.concatenate([turned, jnp.ones((acc.shape[1] - width, rows), jnp.bfloat16)], axis=0)
        mixed = lax.dot_general(turned, weight, DOT, preferred_element_type=jnp.float32)
        acc[n] = acc[n] * jnp.exp2((before - top) * scale) + mixed
        peak[n] = top

    def run(units, mask=None):
        chunk, g, m = units[0]
        scores[0][...] = score(chunk, g, m)
        for i, (chunk, g, m) in enumerate(units):
            if i + 1 < len(units):
                scores[(i + 1) % 2][...] = score(*units[i + 1])
            fold(chunk, g, m, scores[i % 2][...], mask)

    key_row = lax.broadcasted_iota(jnp.int32, (rows, rows), 0)
    query_row = lax.broadcasted_iota(jnp.int32, (rows, rows), 1)

    def diagonal(g, carry):
        mask = (key_row <= query_row) & ((c * rows + key_row < length) | (key_row == 0))
        run([(own.at[g], g, m) for m in range(members)], mask)
        return carry

    lax.fori_loop(0, groups, diagonal, 0)

    def lane_block(lane, i):
        near, far = half * ring, (1 - half) * ring
        ahead_block = jnp.where(
            i < 4, near + (y + ring - 1) % ring, jnp.where(i < 8, near + (y + 2) % ring, far + (y + 2) % ring)
        )
        behind_block = jnp.where(
            i < 4, near + (y + 1) % ring, jnp.where(i < 8, far + (y + 1) % ring, far + (y + 2) % ring)
        )
        across_block = jnp.where(i < 5, far + y, far + (y + ring - 1) % ring)
        block = jnp.where(lane == 0, ahead_block, jnp.where(lane == 1, behind_block, across_block))
        ahead_head = jnp.where(i < 8, i % 4, i - 6)
        across_head = jnp.where(i < 5, (i + 3) % 4, (i + 1) % 4)
        head = jnp.where(lane == 0, ahead_head, jnp.where(lane == 1, i % 4, across_head))
        return block, head

    def arrived(lane, i):
        put(inbox.at[lane, i], inbox.at[lane, i], lane, i, link_recv.at[lane, i], ahead).wait_recv()

    def hand_copy(k):
        target = (c + k) % blocks
        return pltpu.make_async_remote_copy(
            src_ref=chosen.at[pl.ds(2 * target, 2)], dst_ref=cache_ref.at[:, :, 0, c],
            send_sem=hand_send.at[target], recv_sem=hand_recv.at[c],
            device_id=(p, target), device_id_type=MESH,
        )

    def round_trip(i, carry):
        arrived(0, i)
        send_ahead(i + 2)
        send_beside(i + 2)

        @pl.when(i < CROSS)
        def _():
            put(relay.at[i], relay.at[i], 2, i, relay_recv.at[i], beside).wait_recv()
            send_across(i)

        arrived(1, i)
        send_behind(i + 2)

        crossing = (i >= 1) & (i <= CROSS)

        @pl.when(crossing)
        def _():
            arrived(2, i)

        @pl.when(i == CROSS)
        def _():
            def collect(k, inner):
                source = (p + k) % prompts
                pltpu.make_async_remote_copy(
                    src_ref=spread.at[source], dst_ref=gathered.at[source], send_sem=spread_send.at[source],
                    recv_sem=spread_recv.at[source], device_id=(source, c), device_id_type=MESH,
                ).wait_recv()
                return inner

            lax.fori_loop(1, prompts, collect, 0)
            for b in range(chosen.shape[0]):
                chosen[b] = gathered[partner_ref[b]]

            cache_ref[:, :, 0, c] = chosen[pl.ds(2 * c, 2)]

            def hand_start(k, inner):
                hand_copy(k).start()
                return inner

            lax.fori_loop(1, blocks, hand_start, 0)

        places = [lane_block(lane, i) for lane in range(3)]
        every = crossing & (places[0][0] < c) & (places[1][0] < c) & (places[2][0] < c)

        @pl.when(every)
        def _():
            run([(inbox.at[lane, i], places[lane][1], m) for lane in range(3) for m in range(members)])

        @pl.when(jnp.logical_not(every))
        def _():
            def one(lane, inner):
                block, g = lane_block(lane, i)

                @pl.when((block < c) & ((lane < 2) | crossing))
                def _():
                    run([(inbox.at[lane, i], g, m) for m in range(members)])

                return inner

            lax.fori_loop(0, 3, one, 0)

        return carry

    lax.fori_loop(0, ROUNDS, round_trip, 0)

    live = c * rows + lax.broadcasted_iota(jnp.int32, (rows, width), 0) < length

    def finish(n, carry):
        total = acc[n]
        mixture = (total[0:width] / total[width : width + 1]).T
        o_ref[n] = jnp.where(live, mixture, 0.0).astype(jnp.bfloat16)
        return carry

    lax.fori_loop(0, heads, finish, 0)

    def sent(i, carry):
        for lane in range(2):
            put(inbox.at[lane, i], inbox.at[lane, i], lane, i, link_recv.at[lane, i], ahead).wait_send()

        @pl.when(i < CROSS)
        def _():
            for lane in range(2, 4):
                put(relay.at[i], relay.at[i], lane, i, relay_recv.at[i], beside).wait_send()

        return carry

    lax.fori_loop(0, ROUNDS, sent, 0)

    def spread_done(k, carry):
        spread_copy((p + k) % prompts).wait_send()
        return carry

    lax.fori_loop(1, prompts, spread_done, 0)

    def hand_done(k, carry):
        hand_copy(k).wait_send()
        source = (c + k) % blocks
        pltpu.make_async_remote_copy(
            src_ref=chosen.at[pl.ds(2 * source, 2)], dst_ref=cache_ref.at[:, :, 0, source],
            send_sem=hand_send.at[source], recv_sem=hand_recv.at[source],
            device_id=(p, source), device_id_type=MESH,
        ).wait_recv()
        return carry

    lax.fori_loop(1, blocks, hand_done, 0)


def per_device(queries, keys, values, spans, partner):
    rows, heads, width = queries.shape
    groups = keys.shape[1]
    prompts, blocks = lax.axis_size("prompt"), lax.axis_size("ctx")
    stripe_rows = rows * groups // prompts
    vmem, smem = pl.BlockSpec(memory_space=pltpu.VMEM), pl.BlockSpec(memory_space=pltpu.SMEM)
    bf16, f32, dma = jnp.bfloat16, jnp.float32, pltpu.SemaphoreType.DMA
    piece = (2, stripe_rows, width)
    attended, cache = pl.pallas_call(
        fused_kernel,
        out_shape=(
            jax.ShapeDtypeStruct((heads, rows, width), bf16),
            jax.ShapeDtypeStruct((2, 2, 1, blocks, stripe_rows, width), bf16),
        ),
        in_specs=[smem, smem, vmem, vmem, vmem],
        out_specs=(vmem, vmem),
        scratch_shapes=[
            pltpu.VMEM((groups, 2 * rows, width), bf16),
            pltpu.VMEM((3, ROUNDS, 2 * rows, width), bf16),
            pltpu.VMEM((CROSS, 2 * rows, width), bf16),
            pltpu.VMEM((heads, width, rows), bf16),
            pltpu.VMEM((heads, 1, rows), f32),
            pltpu.VMEM((heads, width + 16, rows), f32),
            pltpu.VMEM((rows, rows), f32),
            pltpu.VMEM((rows, rows), f32),
            pltpu.VMEM((prompts,) + piece, bf16),
            pltpu.VMEM((prompts,) + piece, bf16),
            pltpu.VMEM((prompts,) + piece, bf16),
            pltpu.VMEM((rows, width), f32),
            dma((4, ROUNDS)),
            dma((3, ROUNDS)),
            dma((CROSS,)),
            dma((prompts,)),
            dma((prompts,)),
            dma((blocks,)),
            dma((blocks,)),
        ],
        compiler_params=pltpu.CompilerParams(
            collective_id=0, has_side_effects=True, vmem_limit_bytes=56 << 20
        ),
    )(
        spans[:, 0] + spans[:, 1],
        partner,
        queries.transpose(1, 0, 2),
        keys.transpose(1, 0, 2),
        values.transpose(1, 0, 2),
    )
    return attended.transpose(1, 0, 2), cache


def solution(mesh):
    placed = (
        P(("prompt", "ctx"), None, None),
        P(("prompt", "ctx"), None, None),
        P(("prompt", "ctx"), None, None),
        P("prompt", None),
        P(),
    )
    return jax.shard_map(
        per_device,
        mesh=mesh,
        in_specs=placed,
        out_specs=(P(("prompt", "ctx"), None, None), P("ctx", None, "prompt", None, None, None)),
        check_vma=False,
    )
```

profile of v0, /device:TPU:28, one launch (start us, length us, event | category | flops | bytes accessed | tf_op | source)
XLA Modules:
  0.0 108.1 jit_solution(13493393150800474445)
XLA Ops:
  0.6 0.0 copy-start
  0.6 1.4 %fusion = (s32[1,1]{1,0:T(1,128)}, s32[1,1]{1,0:T(1,128)}) fusion(s32[1,2]{1,0:T(1,128)} %param.8), kind=kLoop, calls=%fused_computation.3 | loop fusion | bytes 16 | tf_op jit(solution)/shard_map/slice | solution.py:354
  3.3 2.3 %copy_bitcast_fusion.1 = (bf16[4,512,128]{2,1,0:T(8,128)(2,1)}, bf16[4,512,128]{2,1,0:T(8,128)(2,1)}) fusion(bf16[512,4,128]{2,1,0:T(4,128)(2,1)} %param.7, bf16[512,4,128]{2,1,0:T(4,128)(2,1)} %param.6), kind=kLoop, calls=%fused_computation.1 | loop fusion | bytes 2097152 | tf_op jit(solution)/shard_map/transpose | solution.py:358
  5.6 0.0 copy-done
  5.6 1.9 %copy.14 = bf16[512,16,128]{2,0,1:T(8,128)(2,1)} copy(bf16[512,16,128]{2,1,0:T(8,128)(2,1)S(1)} %copy-done) | data formatting | bytes 4194304 | tf_op args[0]
  7.5 95.2 %shard_map.68 = (bf16[16,512,128]{2,1,0:T(8,128)(2,1)}, bf16[2,2,1,8,128,128]{5,4,3,2,1,0:T(8,128)(2,1)}) custom-call(s32[1]{0:T(128)} %bitcast.len_ref, s32[16]{0:T(128)} %partner_ref.1, bf16[16,512,128]{2,1,0:T(8,128)(2,1)} %bitcast.9, bf16[4,512,128]{2,1,0:T(8,128)(2,1)} %get-tuple-element.11.k_ref, bf16[4,512,128]{2,1,0:T(8,128)(2,1)} %get-tuple-element.10.v_ref), custom_call_target="tpu_custom_call" | custom-call | tf_op jit(solution)/shard_map/pallas_call | solution.py:321
  102.8 0.0 copy-start.1
  102.8 4.3 %copy.10 = bf16[512,16,128]{2,1,0:T(8,128)(2,1)} copy(bf16[512,16,128]{2,0,1:T(8,128)(2,1)} %bitcast.10) | data formatting | bytes 4194304
  107.1 0.0 copy-done.1
  107.1 1.0 copy.16
Async XLA Ops:
  0.6 5.0 %copy-start = (bf16[512,16,128]{2,1,0:T(8,128)(2,1)S(1)}, bf16[512,16,128]{2,1,0:T(8,128)(2,1)}, u32[]{:S(2)}) copy-start(bf16[512,16,128]{2,1,0:T(8,128)(2,1)} %param.5) | copy-start | bytes 6291460
  102.8 4.4 %copy-start.1 = (bf16[2,2,1,8,128,128]{5,4,3,2,1,0:T(8,128)(2,1)S(1)}, bf16[2,2,1,8,128,128]{5,4,3,2,1,0:T(8,128)(2,1)}, u32[]{:S(2)}) copy-start(bf16[2,2,1,8,128,128]{5,4,3,2,1,0:T(8,128)(2,1)} %get-tuple-element.15) | copy-start | bytes 3145732
where the time goes:
time: 108 us
  Pallas kernels  95.2 us (88%)
  local copies, waits for them, and re-layouts  10.9 us (10%)
  between operations  1.96 us (2%)
    pallas_call x1, Pallas kernels, per_device(): pl.pallas_call(fused_kernel, out_shape=(jax.ShapeDtypeStruct((heads, rows...  95.2 us
    unnamed x7, local copies, waits for them, and re-layouts  7.19 us
    transpose x1, local copies, waits for them, and re-layouts, per_device(): values.transpose(1, 0, 2)  2.29 us

commit v1 on v0

--- a/solution.py
+++ b/solution.py
@@ -12,13 +12,14 @@
 MESH = pl.DeviceIdType.MESH
 ROUNDS = 10
 CROSS = 8
+HAND_ROUND = 8
 DOT = (((1,), (0,)), ((), ()))
 
 
 def fused_kernel(
-    len_ref, partner_ref, q_ref, k_ref, v_ref, o_ref, cache_ref,
-    own, inbox, relay, qt, peak, acc, score_a, score_b, spread, gathered, chosen, wide,
-    link_send, link_recv, relay_recv, spread_send, spread_recv, hand_send, hand_recv,
+    spans_ref, partner_ref, q_ref, k_ref, v_ref, o_ref, cache_ref,
+    own, inbox, qt, peak, acc, score_a, score_b, spread, gathered, chosen, wide,
+    link_send, link_recv, spread_send, spread_recv, hand_send, hand_recv,
 ):
     heads, rows, width = q_ref.shape
     groups = k_ref.shape[0]
@@ -31,12 +32,12 @@
     p, c = lax.axis_index("prompt"), lax.axis_index("ctx")
     ring = blocks // 2
     half, y = c // ring, c % ring
-    flipped = p + 2 - 4 * ((p // 2) % 2)
     ahead = (p, half * ring + (y + 1) % ring)
     behind = (p, half * ring + (y + ring - 1) % ring)
-    beside = (flipped, c)
-    across = (flipped, (1 - half) * ring + y)
-    length = len_ref[0]
+    across = (p, ring + y)
+    length = spans_ref[0, 0] + spans_ref[0, 1]
+    ahead_rounds = jnp.where(half == 0, 8, ROUNDS)
+    behind_rounds = jnp.where(half == 0, 4, ROUNDS)
 
     barrier = pltpu.get_barrier_semaphore()
 
@@ -50,7 +51,6 @@
 
     lax.fori_loop(1, prompts, greet_prompt, 0)
     lax.fori_loop(1, blocks, greet_ctx, 0)
-    pl.semaphore_signal(barrier, inc=1, device_id=across, device_id_type=MESH)
 
     for g in range(groups):
         own[g, 0:rows, :] = k_ref[g]
@@ -58,7 +58,7 @@
             own[g, rows + t * width : rows + (t + 1) * width, :] = v_ref[
                 g, t * width : (t + 1) * width, :
             ].T
-    pl.semaphore_wait(barrier, prompts + blocks - 1)
+    pl.semaphore_wait(barrier, prompts + blocks - 2)
 
     def put(src, dst, lane, i, recv, target):
         return pltpu.make_async_remote_copy(
@@ -75,7 +75,7 @@
         def _():
             put(inbox.at[0, i - 4], inbox.at[0, i], 0, i, link_recv.at[0, i], ahead).start()
 
-        @pl.when((i >= 8) & (i < ROUNDS))
+        @pl.when((i >= 8) & (i < ahead_rounds))
         def _():
             put(inbox.at[2, i - 3], inbox.at[0, i], 0, i, link_recv.at[0, i], ahead).start()
 
@@ -84,30 +84,27 @@
         def _():
             put(own.at[i], inbox.at[1, i], 1, i, link_recv.at[1, i], behind).start()
 
-        @pl.when((i >= 4) & (i < 8))
+        @pl.when((i >= 4) & (i < jnp.minimum(8, behind_rounds)))
         def _():
             put(inbox.at[2, i - 3], inbox.at[1, i], 1, i, link_recv.at[1, i], behind).start()
 
-        @pl.when((i >= 8) & (i < ROUNDS))
+        @pl.when((i >= 8) & (i < behind_rounds))
         def _():
             put(inbox.at[1, i - 4], inbox.at[1, i], 1, i, link_recv.at[1, i], behind).start()
 
-    def send_beside(i):
-        @pl.when(i < 4)
-        def _():
-            put(own.at[i], relay.at[i], 2, i, relay_recv.at[i], beside).start()
-
-        @pl.when((i >= 4) & (i < CROSS))
-        def _():
-            put(inbox.at[0, (i - 2) % 4], relay.at[i], 2, i, relay_recv.at[i], beside).start()
-
     def send_across(i):
-        put(relay.at[i], inbox.at[2, i + 1], 3, i, link_recv.at[2, i + 1], across).start()
+        @pl.when((half == 0) & (i < 4))
+        def _():
+            put(own.at[i], inbox.at[2, i + 1], 2, i, link_recv.at[2, i + 1], across).start()
+
+        @pl.when((half == 0) & (i >= 4) & (i < CROSS))
+        def _():
+            put(inbox.at[0, (i - 2) % 4], inbox.at[2, i + 1], 2, i, link_recv.at[2, i + 1], across).start()
 
     for i in range(2):
         send_ahead(jnp.int32(i))
         send_behind(jnp.int32(i))
-        send_beside(jnp.int32(i))
+        send_across(jnp.int32(i))
 
     position = c * rows + lax.broadcasted_iota(jnp.int32, (rows, width), 0)
     stripes = spread.shape[0] // groups
@@ -204,25 +201,25 @@
         )
 
     def round_trip(i, carry):
-        arrived(0, i)
+        @pl.when(i < ahead_rounds)
+        def _():
+            arrived(0, i)
+
         send_ahead(i + 2)
-        send_beside(i + 2)
-
-        @pl.when(i < CROSS)
-        def _():
-            put(relay.at[i], relay.at[i], 2, i, relay_recv.at[i], beside).wait_recv()
-            send_across(i)
-
-        arrived(1, i)
+        send_across(i + 2)
+
+        @pl.when(i < behind_rounds)
+        def _():
+            arrived(1, i)
+
         send_behind(i + 2)
-
-        crossing = (i >= 1) & (i <= CROSS)
+        crossing = (half == 1) & (i >= 1) & (i <= CROSS)
 
         @pl.when(crossing)
         def _():
             arrived(2, i)
 
-        @pl.when(i == CROSS)
+        @pl.when(i == HAND_ROUND)
         def _():
             def collect(k, inner):
                 source = (p + k) % prompts
@@ -279,14 +276,14 @@
     lax.fori_loop(0, heads, finish, 0)
 
     def sent(i, carry):
-        for lane in range(2):
-            put(inbox.at[lane, i], inbox.at[lane, i], lane, i, link_recv.at[lane, i], ahead).wait_send()
-
-        @pl.when(i < CROSS)
-        def _():
-            for lane in range(2, 4):
-                put(relay.at[i], relay.at[i], lane, i, relay_recv.at[i], beside).wait_send()
-
+        def left(lane, going):
+            @pl.when(going)
+            def _():
+                put(inbox.at[0, i], inbox.at[0, i], lane, i, link_recv.at[0, i], ahead).wait_send()
+
+        left(0, i < ahead_rounds)
+        left(1, i < behind_rounds)
+        left(2, (half == 0) & (i < CROSS))
         return carry
 
     lax.fori_loop(0, ROUNDS, sent, 0)
@@ -329,7 +326,6 @@
         scratch_shapes=[
             pltpu.VMEM((groups, 2 * rows, width), bf16),
             pltpu.VMEM((3, ROUNDS, 2 * rows, width), bf16),
-            pltpu.VMEM((CROSS, 2 * rows, width), bf16),
             pltpu.VMEM((heads, width, rows), bf16),
             pltpu.VMEM((heads, 1, rows), f32),
             pltpu.VMEM((heads, width + 16, rows), f32),
@@ -339,9 +335,8 @@
             pltpu.VMEM((prompts,) + piece, bf16),
             pltpu.VMEM((prompts,) + piece, bf16),
             pltpu.VMEM((rows, width), f32),
-            dma((4, ROUNDS)),
             dma((3, ROUNDS)),
-            dma((CROSS,)),
+            dma((3, ROUNDS)),
             dma((prompts,)),
             dma((prompts,)),
             dma((blocks,)),
@@ -351,7 +346,7 @@
             collective_id=0, has_side_effects=True, vmem_limit_bytes=56 << 20
         ),
     )(
-        spans[:, 0] + spans[:, 1],
+        spans,
         partner,
         queries.transpose(1, 0, 2),
         keys.transpose(1, 0, 2),

time: 108 us -> 93.9 us (0.87)
  the two profiles are of different devices: /device:TPU:28 before, /device:TPU:24 now
where the time goes in v1:
time: 93.9 us; the launch traced here: 93.8 us
  Pallas kernels  83.5 us (89%)
  local copies, waits for them, and re-layouts  9.63 us (10%)
    pallas_call x1, Pallas kernels, per_device(): pl.pallas_call(fused_kernel, out_shape=(jax.ShapeDtypeStruct((heads, rows...  83.5 us
    unnamed x7, local copies, waits for them, and re-layouts  7.19 us
    transpose x1, local copies, waits for them, and re-layouts, per_device(): values.transpose(1, 0, 2)  2.45 us

profile of v1, /device:TPU:24, one launch (start us, length us, event | category | flops | bytes accessed | tf_op | source)
XLA Modules:
  0.0 93.8 jit_solution(4618877754870444051)
XLA Ops:
  0.6 0.0 copy-start
  0.6 2.4 %copy_bitcast_fusion.1 = (bf16[4,512,128]{2,1,0:T(8,128)(2,1)}, bf16[4,512,128]{2,1,0:T(8,128)(2,1)}) fusion(bf16[512,4,128]{2,1,0:T(4,128)(2,1)} %param.7, bf16[512,4,128]{2,1,0:T(4,128)(2,1)} %param.6), kind=kLoop, calls=%fused_computation.1 | loop fusion | bytes 2097152 | tf_op jit(solution)/shard_map/transpose | solution.py:353
  3.1 0.0 copy-done
  3.1 1.9 %copy.14 = bf16[512,16,128]{2,0,1:T(8,128)(2,1)} copy(bf16[512,16,128]{2,1,0:T(8,128)(2,1)S(1)} %copy-done) | data formatting | bytes 4194304 | tf_op args[0]
  4.9 83.5 %shard_map.68 = (bf16[16,512,128]{2,1,0:T(8,128)(2,1)}, bf16[2,2,1,8,128,128]{5,4,3,2,1,0:T(8,128)(2,1)}) custom-call(s32[1,2]{1,0:T(1,128)} %spans_ref.1, s32[16]{0:T(128)} %partner_ref.1, bf16[16,512,128]{2,1,0:T(8,128)(2,1)} %bitcast.8, bf16[4,512,128]{2,1,0:T(8,128)(2,1)} %get-tuple-element.9.k_ref, bf16[4,512,128]{2,1,0:T(8,128)(2,1)} %get-tuple-element.8.v_ref), custom_call_target="tpu_custom_call" | custom-call | tf_op jit(solution)/shard_map/pallas_call | solution.py:318
  88.5 0.0 copy-start.1
  88.5 4.3 %copy.10 = bf16[512,16,128]{2,1,0:T(8,128)(2,1)} copy(bf16[512,16,128]{2,0,1:T(8,128)(2,1)} %bitcast.9) | data formatting | bytes 4194304
  92.8 0.0 copy-done.1
  92.8 1.0 %copy.16 = bf16[2,2,1,8,128,128]{5,4,3,2,1,0:T(8,128)(2,1)} copy(bf16[2,2,1,8,128,128]{5,4,3,2,1,0:T(8,128)(2,1)S(1)} %copy-done.1) | data formatting | bytes 2097152
Async XLA Ops:
  0.6 2.5 %copy-start = (bf16[512,16,128]{2,1,0:T(8,128)(2,1)S(1)}, bf16[512,16,128]{2,1,0:T(8,128)(2,1)}, u32[]{:S(2)}) copy-start(bf16[512,16,128]{2,1,0:T(8,128)(2,1)} %param.5) | copy-start | bytes 6291460
  88.5 4.4 %copy-start.1 = (bf16[2,2,1,8,128,128]{5,4,3,2,1,0:T(8,128)(2,1)S(1)}, bf16[2,2,1,8,128,128]{5,4,3,2,1,0:T(8,128)(2,1)}, u32[]{:S(2)}) copy-start(bf16[2,2,1,8,128,128]{5,4,3,2,1,0:T(8,128)(2,1)} %get-tuple-element.13) | copy-start | bytes 3145732

commit v2 on v1

--- a/solution.py
+++ b/solution.py
@@ -12,17 +12,18 @@
 MESH = pl.DeviceIdType.MESH
 ROUNDS = 10
 CROSS = 8
-HAND_ROUND = 8
+HAND_ROUND = 5
+LATE_ROUND = 8
 DOT = (((1,), (0,)), ((), ()))
 
 
 def fused_kernel(
     spans_ref, partner_ref, q_ref, k_ref, v_ref, o_ref, cache_ref,
-    own, inbox, qt, peak, acc, score_a, score_b, spread, gathered, chosen, wide,
-    link_send, link_recv, spread_send, spread_recv, hand_send, hand_recv,
+    own, plain, raw, turned, inbox, qt, peak, acc, score_a, score_b, spread, gathered, chosen, via, wide,
+    link_send, link_recv, spread_send, spread_recv, hand_send, hand_recv, via_send, via_recv, raw_sem,
 ):
-    heads, rows, width = q_ref.shape
-    groups = k_ref.shape[0]
+    rows, heads, width = q_ref.shape
+    groups = k_ref.shape[1]
     members = heads // groups
     tiles = rows // width
     scale = LOG2E / math.sqrt(width)
@@ -52,12 +53,17 @@
     lax.fori_loop(1, prompts, greet_prompt, 0)
     lax.fori_loop(1, blocks, greet_ctx, 0)
 
-    for g in range(groups):
-        own[g, 0:rows, :] = k_ref[g]
-        for t in range(tiles):
-            own[g, rows + t * width : rows + (t + 1) * width, :] = v_ref[
-                g, t * width : (t + 1) * width, :
-            ].T
+    fetch = pltpu.make_async_copy(q_ref, raw, raw_sem)
+    fetch.start()
+
+    for t in range(tiles):
+        part = slice(t * width, (t + 1) * width)
+        by_head = jnp.swapaxes(k_ref[part], 0, 1)
+        values_by_head = jnp.swapaxes(v_ref[part], 0, 1)
+        for g in range(groups):
+            own[g, part, :] = by_head[g]
+            plain[g, part, :] = values_by_head[g]
+            own[g, rows + t * width : rows + (t + 1) * width, :] = values_by_head[g].T
     pl.semaphore_wait(barrier, prompts + blocks - 2)
 
     def put(src, dst, lane, i, recv, target):
@@ -66,52 +72,49 @@
             device_id=target, device_id_type=MESH,
         )
 
-    def send_ahead(i):
-        @pl.when(i < 4)
-        def _():
-            put(own.at[i], inbox.at[0, i], 0, i, link_recv.at[0, i], ahead).start()
-
-        @pl.when((i >= 4) & (i < 8))
-        def _():
-            put(inbox.at[0, i - 4], inbox.at[0, i], 0, i, link_recv.at[0, i], ahead).start()
-
-        @pl.when((i >= 8) & (i < ahead_rounds))
-        def _():
-            put(inbox.at[2, i - 3], inbox.at[0, i], 0, i, link_recv.at[0, i], ahead).start()
-
-    def send_behind(i):
-        @pl.when(i < 4)
-        def _():
-            put(own.at[i], inbox.at[1, i], 1, i, link_recv.at[1, i], behind).start()
-
-        @pl.when((i >= 4) & (i < jnp.minimum(8, behind_rounds)))
-        def _():
-            put(inbox.at[2, i - 3], inbox.at[1, i], 1, i, link_recv.at[1, i], behind).start()
-
-        @pl.when((i >= 8) & (i < behind_rounds))
-        def _():
-            put(inbox.at[1, i - 4], inbox.at[1, i], 1, i, link_recv.at[1, i], behind).start()
-
-    def send_across(i):
-        @pl.when((half == 0) & (i < 4))
-        def _():
-            put(own.at[i], inbox.at[2, i + 1], 2, i, link_recv.at[2, i + 1], across).start()
-
-        @pl.when((half == 0) & (i >= 4) & (i < CROSS))
-        def _():
-            put(inbox.at[0, (i - 2) % 4], inbox.at[2, i + 1], 2, i, link_recv.at[2, i + 1], across).start()
-
-    for i in range(2):
-        send_ahead(jnp.int32(i))
-        send_behind(jnp.int32(i))
-        send_across(jnp.int32(i))
+    def send_ahead(src, i):
+        put(src, inbox.at[0, i], 0, i, link_recv.at[0, i], ahead).start()
+
+    def send_behind(src, i):
+        put(src, inbox.at[1, i], 1, i, link_recv.at[1, i], behind).start()
+
+    def send_across(src, i):
+        put(src, inbox.at[2, i + 1], 2, i, link_recv.at[2, i + 1], across).start()
+
+    for i in range(groups):
+        send_ahead(own.at[i], i)
+        send_behind(own.at[i], i)
+
+        @pl.when(half == 0)
+        def _():
+            send_across(own.at[i], i)
+
+    fetch.wait()
+    cut = 64
+
+    def sort_heads(b, carry):
+        first = pl.multiple_of(b * cut, cut)
+        by_head = jnp.swapaxes(raw[pl.ds(first, cut)], 0, 1)
+        for n in range(heads):
+            turned[n, pl.ds(first, cut), :] = by_head[n]
+        return carry
+
+    lax.fori_loop(0, rows // cut, sort_heads, 0)
+
+    def turn(n, carry):
+        qt[n] = turned[n].T
+        peak[n] = jnp.full((1, rows), -1e30, jnp.float32)
+        acc[n] = jnp.zeros(acc.shape[1:], jnp.float32)
+        return carry
+
+    lax.fori_loop(0, heads, turn, 0)
 
     position = c * rows + lax.broadcasted_iota(jnp.int32, (rows, width), 0)
     stripes = spread.shape[0] // groups
     stripe_rows = rows // stripes
-    for part, ref in enumerate((k_ref, v_ref)):
+    for part, ref in enumerate((own, plain)):
         for g in range(groups):
-            wide[...] = jnp.where(position < length, ref[g].astype(jnp.float32), 0.0)
+            wide[...] = jnp.where(position < length, ref[g, 0:rows].astype(jnp.float32), 0.0)
             for st in range(stripes):
                 spread[st * groups + g, part] = wide[pl.ds(st, stripe_rows, stride=stripes), :].astype(jnp.bfloat16)
 
@@ -127,14 +130,6 @@
 
     gathered[p] = spread[p]
     lax.fori_loop(1, prompts, spread_start, 0)
-
-    def turn(n, carry):
-        qt[n] = q_ref[n].T
-        peak[n] = jnp.full((1, rows), -1e30, jnp.float32)
-        acc[n] = jnp.zeros(acc.shape[1:], jnp.float32)
-        return carry
-
-    lax.fori_loop(0, heads, turn, 0)
 
     def score(chunk, g, m):
         return lax.dot_general(
@@ -184,40 +179,65 @@
         )
         across_block = jnp.where(i < 5, far + y, far + (y + ring - 1) % ring)
         block = jnp.where(lane == 0, ahead_block, jnp.where(lane == 1, behind_block, across_block))
-        ahead_head = jnp.where(i < 8, i % 4, i - 6)
-        across_head = jnp.where(i < 5, (i + 3) % 4, (i + 1) % 4)
-        head = jnp.where(lane == 0, ahead_head, jnp.where(lane == 1, i % 4, across_head))
+        behind_head = jnp.where(i < 8, i % 4, i - 6)
+        head = jnp.where(lane == 0, i % 4, jnp.where(lane == 1, behind_head, (i + 3) % 4))
         return block, head
 
     def arrived(lane, i):
         put(inbox.at[lane, i], inbox.at[lane, i], lane, i, link_recv.at[lane, i], ahead).wait_recv()
 
-    def hand_copy(k):
-        target = (c + k) % blocks
+    def hand_copy(rows_of, sem, dst, recv, target):
         return pltpu.make_async_remote_copy(
-            src_ref=chosen.at[pl.ds(2 * target, 2)], dst_ref=cache_ref.at[:, :, 0, c],
-            send_sem=hand_send.at[target], recv_sem=hand_recv.at[c],
-            device_id=(p, target), device_id_type=MESH,
-        )
+            src_ref=chosen.at[pl.ds(2 * rows_of, 2)], dst_ref=dst, send_sem=hand_send.at[sem],
+            recv_sem=recv, device_id=(p, target), device_id_type=MESH,
+        )
+
+    def hand_direct(target):
+        hand_copy(target, target, cache_ref.at[:, :, 0, c], hand_recv.at[c], target).start()
+
+    def forward_copy(source):
+        return pltpu.make_async_remote_copy(
+            src_ref=via.at[source], dst_ref=cache_ref.at[:, :, 0, source], send_sem=via_send.at[source],
+            recv_sem=hand_recv.at[source], device_id=(p, ring + y), device_id_type=MESH,
+        )
+
+    def via_copy(beside):
+        return hand_copy(ring + beside, ring + beside, via.at[y], via_recv.at[y], beside)
 
     def round_trip(i, carry):
         @pl.when(i < ahead_rounds)
         def _():
             arrived(0, i)
 
-        send_ahead(i + 2)
-        send_across(i + 2)
+        @pl.when(i < 4)
+        def _():
+            send_ahead(inbox.at[0, i], i + 4)
+
+            @pl.when(half == 0)
+            def _():
+                send_across(inbox.at[0, i], i + 4)
 
         @pl.when(i < behind_rounds)
         def _():
             arrived(1, i)
 
-        send_behind(i + 2)
+        @pl.when((half == 1) & (i >= 6) & (i < 8))
+        def _():
+            send_behind(inbox.at[1, i], i + 2)
+
         crossing = (half == 1) & (i >= 1) & (i <= CROSS)
 
         @pl.when(crossing)
         def _():
             arrived(2, i)
+
+            @pl.when(i <= 4)
+            def _():
+                send_behind(inbox.at[2, i], i + 3)
+
+            @pl.when((i >= 5) & (i <= 6))
+            def _():
+                send_ahead(inbox.at[2, i], i + 3)
 
         @pl.when(i == HAND_ROUND)
         def _():
@@ -232,14 +252,47 @@
             lax.fori_loop(1, prompts, collect, 0)
             for b in range(chosen.shape[0]):
                 chosen[b] = gathered[partner_ref[b]]
-
             cache_ref[:, :, 0, c] = chosen[pl.ds(2 * c, 2)]
 
-            def hand_start(k, inner):
-                hand_copy(k).start()
+            @pl.when(half == 0)
+            def _():
+                hand_direct(ring + y)
+
+                def beside_start(k, inner):
+                    via_copy((y + k) % ring).start()
+                    hand_direct((y + k) % ring)
+                    return inner
+
+                lax.fori_loop(1, ring, beside_start, 0)
+
+            @pl.when(half == 1)
+            def _():
+                def across_start(k, inner):
+                    hand_direct((y + k) % ring)
+                    return inner
+
+                lax.fori_loop(0, ring, across_start, 0)
+
+        @pl.when((i == LATE_ROUND) & (half == 1))
+        def _():
+            def near_start(k, inner):
+                hand_direct(ring + (y + k) % ring)
                 return inner
 
-            lax.fori_loop(1, blocks, hand_start, 0)
+            lax.fori_loop(1, ring, near_start, 0)
+
+        @pl.when((i == LATE_ROUND) & (half == 0))
+        def _():
+            def forward(k, inner):
+                source = (y + k) % ring
+                pltpu.make_async_remote_copy(
+                    src_ref=via.at[source], dst_ref=via.at[source], send_sem=via_send.at[source],
+                    recv_sem=via_recv.at[source], device_id=(p, source), device_id_type=MESH,
+                ).wait_recv()
+                forward_copy(source).start()
+                return inner
+
+            lax.fori_loop(1, ring, forward, 0)
 
         places = [lane_block(lane, i) for lane in range(3)]
         every = crossing & (places[0][0] < c) & (places[1][0] < c) & (places[2][0] < c)
@@ -270,10 +323,17 @@
     def finish(n, carry):
         total = acc[n]
         mixture = (total[0:width] / total[width : width + 1]).T
-        o_ref[n] = jnp.where(live, mixture, 0.0).astype(jnp.bfloat16)
+        turned[n] = jnp.where(live, mixture, 0.0).astype(jnp.bfloat16)
         return carry
 
     lax.fori_loop(0, heads, finish, 0)
+
+    def sort_rows(b, carry):
+        first = pl.multiple_of(b * cut, cut)
+        o_ref[pl.ds(first, cut)] = jnp.swapaxes(turned[:, pl.ds(first, cut), :], 0, 1)
+        return carry
+
+    lax.fori_loop(0, rows // cut, sort_rows, 0)
 
     def sent(i, carry):
         def left(lane, going):
@@ -294,14 +354,19 @@
 
     lax.fori_loop(1, prompts, spread_done, 0)
 
+    @pl.when(half == 0)
+    def _():
+        def forwarded(k, carry):
+            forward_copy((y + k) % ring).wait_send()
+            return carry
+
+        lax.fori_loop(1, ring, forwarded, 0)
+
     def hand_done(k, carry):
-        hand_copy(k).wait_send()
-        source = (c + k) % blocks
-        pltpu.make_async_remote_copy(
-            src_ref=chosen.at[pl.ds(2 * source, 2)], dst_ref=cache_ref.at[:, :, 0, source],
-            send_sem=hand_send.at[source], recv_sem=hand_recv.at[source],
-            device_id=(p, source), device_id_type=MESH,
-        ).wait_recv()
+        other = (c + k) % blocks
+        done = hand_copy(other, other, cache_ref.at[:, :, 0, other], hand_recv.at[other], other)
+        done.wait_send()
+        done.wait_recv()
         return carry
 
     lax.fori_loop(1, blocks, hand_done, 0)
@@ -315,16 +380,19 @@
     vmem, smem = pl.BlockSpec(memory_space=pltpu.VMEM), pl.BlockSpec(memory_space=pltpu.SMEM)
     bf16, f32, dma = jnp.bfloat16, jnp.float32, pltpu.SemaphoreType.DMA
     piece = (2, stripe_rows, width)
-    attended, cache = pl.pallas_call(
+    return pl.pallas_call(
         fused_kernel,
         out_shape=(
-            jax.ShapeDtypeStruct((heads, rows, width), bf16),
+            jax.ShapeDtypeStruct((rows, heads, width), bf16),
             jax.ShapeDtypeStruct((2, 2, 1, blocks, stripe_rows, width), bf16),
         ),
-        in_specs=[smem, smem, vmem, vmem, vmem],
+        in_specs=[smem, smem, pl.BlockSpec(memory_space=pl.ANY), vmem, vmem],
         out_specs=(vmem, vmem),
         scratch_shapes=[
             pltpu.VMEM((groups, 2 * rows, width), bf16),
+            pltpu.VMEM((groups, rows, width), bf16),
+            pltpu.VMEM((rows, heads, width), bf16),
+            pltpu.VMEM((heads, rows, width), bf16),
             pltpu.VMEM((3, ROUNDS, 2 * rows, width), bf16),
             pltpu.VMEM((heads, width, rows), bf16),
             pltpu.VMEM((heads, 1, rows), f32),
@@ -334,6 +402,7 @@
             pltpu.VMEM((prompts,) + piece, bf16),
             pltpu.VMEM((prompts,) + piece, bf16),
             pltpu.VMEM((prompts,) + piece, bf16),
+            pltpu.VMEM((blocks // 2, 2) + piece, bf16),
             pltpu.VMEM((rows, width), f32),
             dma((3, ROUNDS)),
             dma((3, ROUNDS)),
@@ -341,18 +410,14 @@
             dma((prompts,)),
             dma((blocks,)),
             dma((blocks,)),
+            dma((blocks // 2,)),
+            dma((blocks // 2,)),
+            dma,
         ],
         compiler_params=pltpu.CompilerParams(
             collective_id=0, has_side_effects=True, vmem_limit_bytes=56 << 20
         ),
-    )(
-        spans,
-        partner,
-        queries.transpose(1, 0, 2),
-        keys.transpose(1, 0, 2),
-        values.transpose(1, 0, 2),
-    )
-    return attended.transpose(1, 0, 2), cache
+    )(spans, partner, queries, keys, values)
 
 
 def solution(mesh):

time: 93.9 us -> 83.8 us (0.89)
  the two profiles are of different devices: /device:TPU:24 before, /device:TPU:28 now
where the time goes in v2:
time: 83.8 us; the launch traced here: 83.2 us
  Pallas kernels  78.2 us (93%)
  local copies, waits for them, and re-layouts  4.33 us (5%)
    pallas_call x1, Pallas kernels, per_device(): pl.pallas_call(fused_kernel, out_shape=(jax.ShapeDtypeStruct((rows, heads...  78.2 us
    unnamed x4, local copies, waits for them, and re-layouts  4.33 us

profile of v2, /device:TPU:28, one launch (start us, length us, event | category | flops | bytes accessed | tf_op | source)
XLA Modules:
  0.0 83.2 jit_solution(15527467693472346846)
XLA Ops:
  0.6 78.2 %shard_map.68 = (bf16[512,16,128]{2,1,0:T(8,128)(2,1)}, bf16[2,2,1,8,128,128]{5,4,3,2,1,0:T(8,128)(2,1)}) custom-call(s32[1,2]{1,0:T(1,128)} %spans_ref.1, s32[16]{0:T(128)} %partner_ref.1, bf16[512,16,128]{2,1,0:T(8,128)(2,1)} %q_ref.1, bf16[512,4,128]{2,1,0:T(4,128)(2,1)} %k_ref.1, bf16[512,4,128]{2,1,0:T(4,128)(2,1)} %v_ref.1), custom_call_target="tpu_custom_call" | custom-call | tf_op jit(solution)/shard_map/pallas_call | solution.py:383
  78.9 0.0 copy-start
  78.9 3.4 %copy.9 = bf16[512,16,128]{2,1,0:T(8,128)(2,1)} copy(bf16[512,16,128]{2,1,0:T(8,128)(2,1)} %get-tuple-element.4) | data formatting | bytes 4194304
  82.2 0.0 copy-done
  82.2 1.0 %copy.10 = bf16[2,2,1,8,128,128]{5,4,3,2,1,0:T(8,128)(2,1)} copy(bf16[2,2,1,8,128,128]{5,4,3,2,1,0:T(8,128)(2,1)S(1)} %copy-done) | data formatting | bytes 2097152
Async XLA Ops:
  78.9 3.4 %copy-start = (bf16[2,2,1,8,128,128]{5,4,3,2,1,0:T(8,128)(2,1)S(1)}, bf16[2,2,1,8,128,128]{5,4,3,2,1,0:T(8,128)(2,1)}, u32[]{:S(2)}) copy-start(bf16[2,2,1,8,128,128]{5,4,3,2,1,0:T(8,128)(2,1)} %get-tuple-element.5) | copy-start | bytes 3145732

commit v3 on v2

--- a/solution.py
+++ b/solution.py
@@ -20,7 +20,7 @@
 def fused_kernel(
     spans_ref, partner_ref, q_ref, k_ref, v_ref, o_ref, cache_ref,
     own, plain, raw, turned, inbox, qt, peak, acc, score_a, score_b, spread, gathered, chosen, via, wide,
-    link_send, link_recv, spread_send, spread_recv, hand_send, hand_recv, via_send, via_recv, raw_sem,
+    link_send, link_recv, spread_send, spread_recv, hand_send, hand_recv, via_send, via_recv, raw_sem, out_sem, word,
 ):
     rows, heads, width = q_ref.shape
     groups = k_ref.shape[1]
@@ -40,18 +40,25 @@
     ahead_rounds = jnp.where(half == 0, 8, ROUNDS)
     behind_rounds = jnp.where(half == 0, 4, ROUNDS)
 
+    near = (
+        ((p + 4) % prompts, c),
+        ((p + prompts - 4) % prompts, c),
+        (p + 2 - 4 * ((p // 2) % 2), c),
+        (p + 1 - 2 * (p % 2), c),
+        ahead,
+        behind,
+        (p, (1 - half) * ring + y),
+    )
     barrier = pltpu.get_barrier_semaphore()
-
-    def greet_prompt(k, carry):
-        pl.semaphore_signal(barrier, inc=1, device_id=((p + k) % prompts, c), device_id_type=MESH)
-        return carry
-
-    def greet_ctx(k, carry):
-        pl.semaphore_signal(barrier, inc=1, device_id=(p, (c + k) % blocks), device_id_type=MESH)
-        return carry
-
-    lax.fori_loop(1, prompts, greet_prompt, 0)
-    lax.fori_loop(1, blocks, greet_ctx, 0)
+    for device in near:
+        pl.semaphore_signal(barrier, inc=1, device_id=device, device_id_type=MESH)
+
+    def pass_word(stage):
+        for device in near[:4]:
+            pl.semaphore_signal(word.at[stage], inc=1, device_id=device, device_id_type=MESH)
+
+    def hear_word(stage):
+        pl.semaphore_wait(word.at[stage], 4)
 
     fetch = pltpu.make_async_copy(q_ref, raw, raw_sem)
     fetch.start()
@@ -64,7 +71,8 @@
             own[g, part, :] = by_head[g]
             plain[g, part, :] = values_by_head[g]
             own[g, rows + t * width : rows + (t + 1) * width, :] = values_by_head[g].T
-    pl.semaphore_wait(barrier, prompts + blocks - 2)
+    pl.semaphore_wait(barrier, len(near))
+    pass_word(0)
 
     def put(src, dst, lane, i, recv, target):
         return pltpu.make_async_remote_copy(
@@ -90,6 +98,8 @@
             send_across(own.at[i], i)
 
     fetch.wait()
+    hear_word(0)
+    pass_word(1)
     cut = 64
 
     def sort_heads(b, carry):
@@ -107,6 +117,8 @@
         acc[n] = jnp.zeros(acc.shape[1:], jnp.float32)
         return carry
 
+    hear_word(1)
+    pass_word(2)
     lax.fori_loop(0, heads, turn, 0)
 
     position = c * rows + lax.broadcasted_iota(jnp.int32, (rows, width), 0)
@@ -129,6 +141,7 @@
         return carry
 
     gathered[p] = spread[p]
+    hear_word(2)
     lax.fori_loop(1, prompts, spread_start, 0)
 
     def score(chunk, g, m):
@@ -204,7 +217,25 @@
     def via_copy(beside):
         return hand_copy(ring + beside, ring + beside, via.at[y], via_recv.at[y], beside)
 
+    live = c * rows + lax.broadcasted_iota(jnp.int32, (width, rows), 1) < length
+
+    def finish(n):
+        total = acc[n]
+        mixture = total[0:width] * (1.0 / total[width : width + 1])
+        turned[n] = jnp.where(live, mixture, 0.0).astype(jnp.bfloat16).T
+
+    def early_head(k):
+        return (k // members) * 2 * members + k % members
+
     def round_trip(i, carry):
+        @pl.when(i == ROUNDS - 1)
+        def _():
+            def early_finish(k, inner):
+                finish(early_head(k))
+                return inner
+
+            lax.fori_loop(0, heads // 2, early_finish, 0)
+
         @pl.when(i < ahead_rounds)
         def _():
             arrived(0, i)
@@ -318,22 +349,25 @@
 
     lax.fori_loop(0, ROUNDS, round_trip, 0)
 
-    live = c * rows + lax.broadcasted_iota(jnp.int32, (rows, width), 0) < length
-
-    def finish(n, carry):
-        total = acc[n]
-        mixture = (total[0:width] / total[width : width + 1]).T
-        turned[n] = jnp.where(live, mixture, 0.0).astype(jnp.bfloat16)
-        return carry
-
-    lax.fori_loop(0, heads, finish, 0)
-
-    def sort_rows(b, carry):
-        first = pl.multiple_of(b * cut, cut)
-        o_ref[pl.ds(first, cut)] = jnp.swapaxes(turned[:, pl.ds(first, cut), :], 0, 1)
-        return carry
-
-    lax.fori_loop(0, rows // cut, sort_rows, 0)
+    def leave(n):
+        return pltpu.make_async_copy(turned.at[n], o_ref.at[n], out_sem.at[n])
+
+    def early_leave(k, carry):
+        leave(early_head(k)).start()
+        return carry
+
+    lax.fori_loop(0, heads // 2, early_leave, 0)
+
+    def late_finish(k, carry):
+        finish(early_head(k) + members)
+
+        @pl.when(k > 0)
+        def _():
+            leave(early_head(k - 1) + members).start()
+
+        return carry
+
+    lax.fori_loop(0, heads // 2, late_finish, 0)
 
     def sent(i, carry):
         def left(lane, going):
@@ -347,6 +381,13 @@
         return carry
 
     lax.fori_loop(0, ROUNDS, sent, 0)
+    leave(heads - 1).start()
+
+    def left_for_good(n, carry):
+        leave(n).wait()
+        return carry
+
+    lax.fori_loop(0, heads, left_for_good, 0)
 
     def spread_done(k, carry):
         spread_copy((p + k) % prompts).wait_send()
@@ -370,6 +411,11 @@
         return carry
 
     lax.fori_loop(1, blocks, hand_done, 0)
+
+
+def place_kernel(head_ref, cache_in, o_ref, cache_out):
+    o_ref[...] = jnp.swapaxes(head_ref[...], 0, 1)
+    cache_out[...] = cache_in[...]
 
 
 def per_device(queries, keys, values, spans, partner):
@@ -380,14 +426,14 @@
     vmem, smem = pl.BlockSpec(memory_space=pltpu.VMEM), pl.BlockSpec(memory_space=pltpu.SMEM)
     bf16, f32, dma = jnp.bfloat16, jnp.float32, pltpu.SemaphoreType.DMA
     piece = (2, stripe_rows, width)
-    return pl.pallas_call(
+    by_head, cache = pl.pallas_call(
         fused_kernel,
         out_shape=(
-            jax.ShapeDtypeStruct((rows, heads, width), bf16),
+            jax.ShapeDtypeStruct((heads, rows, width), bf16),
             jax.ShapeDtypeStruct((2, 2, 1, blocks, stripe_rows, width), bf16),
         ),
         in_specs=[smem, smem, pl.BlockSpec(memory_space=pl.ANY), vmem, vmem],
-        out_specs=(vmem, vmem),
+        out_specs=(pl.BlockSpec(memory_space=pl.ANY), vmem),
         scratch_shapes=[
             pltpu.VMEM((groups, 2 * rows, width), bf16),
             pltpu.VMEM((groups, rows, width), bf16),
@@ -413,11 +459,23 @@
             dma((blocks // 2,)),
             dma((blocks // 2,)),
             dma,
+            dma((heads,)),
+            pltpu.SemaphoreType.REGULAR((3,)),
         ],
         compiler_params=pltpu.CompilerParams(
             collective_id=0, has_side_effects=True, vmem_limit_bytes=56 << 20
         ),
     )(spans, partner, queries, keys, values)
+    steps = blocks // 4
+    cache_block = pl.BlockSpec((2, 2, 1, 4, stripe_rows, width), lambda i: (0, 0, 0, i, 0, 0))
+    return pl.pallas_call(
+        place_kernel,
+        out_shape=(jax.ShapeDtypeStruct(queries.shape, bf16), jax.ShapeDtypeStruct(cache.shape, bf16)),
+        grid=(steps,),
+        in_specs=[pl.BlockSpec((heads, rows // steps, width), lambda i: (0, i, 0)), cache_block],
+        out_specs=(pl.BlockSpec((rows // steps, heads, width), lambda i: (i, 0, 0)), cache_block),
+        compiler_params=pltpu.CompilerParams(dimension_semantics=("arbitrary",)),
+    )(by_head, cache)
 
 
 def solution(mesh):

time: 83.8 us -> 81.2 us (0.969)
  local copies, waits for them, and re-layouts: 4.33 us -> 0 us
  Pallas kernels: 78.2 us -> 79.3 us
    unnamed x4 -> x0, local copies, waits for them, and re-layouts: 4.33 us -> none
    pallas_call x1 -> x2, Pallas kernels: 78.2 us -> 79.3 us  [the longest x1 75.9 us: per_device(): pl.pallas_call(fused_kernel, out_shape=(jax.ShapeDtypeStruct((heads, rows...]
where the time goes in v3:
time: 81.2 us; the launch traced here: 79.9 us
  Pallas kernels  79.3 us (98%)
    pallas_call x1, Pallas kernels, per_device(): pl.pallas_call(fused_kernel, out_shape=(jax.ShapeDtypeStruct((heads, rows...  75.9 us
    pallas_call x1, Pallas kernels, per_device(): pl.pallas_call(place_kernel, out_shape=(jax.ShapeDtypeStruct(queries.shap...  3.35 us

profile of v3, /device:TPU:28, one launch (start us, length us, event | category | flops | bytes accessed | tf_op | source)
XLA Modules:
  0.0 79.9 jit_solution(10345754816175452664)
XLA Ops:
  0.6 75.9 %shard_map.68 = (bf16[16,512,128]{2,1,0:T(8,128)(2,1)}, bf16[2,2,1,8,128,128]{5,4,3,2,1,0:T(8,128)(2,1)}) custom-call(s32[1,2]{1,0:T(1,128)} %spans_ref.1, s32[16]{0:T(128)} %partner_ref.1, bf16[512,16,128]{2,1,0:T(8,128)(2,1)} %q_ref.1, bf16[512,4,128]{2,1,0:T(4,128)(2,1)} %k_ref.1, bf16[512,4,128]{2,1,0:T(4,128)(2,1)} %v_ref.1), custom_call_target="tpu_custom_call" | custom-call | tf_op jit(solution)/shard_map/pallas_call | solution.py:429
  76.5 3.4 %shard_map.69 = (bf16[512,16,128]{2,1,0:T(8,128)(2,1)}, bf16[2,2,1,8,128,128]{5,4,3,2,1,0:T(8,128)(2,1)}) custom-call(bf16[16,512,128]{2,1,0:T(8,128)(2,1)} %get-tuple-element.4.head_ref, bf16[2,2,1,8,128,128]{5,4,3,2,1,0:T(8,128)(2,1)} %get-tuple-element.5.cache_in), custom_call_target="tpu_custom_call" | custom-call | tf_op jit(solution)/shard_map/pallas_call | solution.py:471

commit v4 on v3

--- a/solution.py
+++ b/solution.py
@@ -37,8 +37,8 @@
     behind = (p, half * ring + (y + ring - 1) % ring)
     across = (p, ring + y)
     length = spans_ref[0, 0] + spans_ref[0, 1]
-    ahead_rounds = jnp.where(half == 0, 8, ROUNDS)
-    behind_rounds = jnp.where(half == 0, 4, ROUNDS)
+    ahead_rounds = jnp.where(half == 0, 6, ROUNDS)
+    behind_rounds = jnp.where(half == 0, 6, ROUNDS)
 
     near = (
         ((p + 4) % prompts, c),
@@ -190,9 +190,11 @@
         behind_block = jnp.where(
             i < 4, near + (y + 1) % ring, jnp.where(i < 8, far + (y + 1) % ring, far + (y + 2) % ring)
         )
+        split = (half == 0) & (i >= 4)
+        behind_block = jnp.where(split, near + (y + 2) % ring, behind_block)
         across_block = jnp.where(i < 5, far + y, far + (y + ring - 1) % ring)
         block = jnp.where(lane == 0, ahead_block, jnp.where(lane == 1, behind_block, across_block))
-        behind_head = jnp.where(i < 8, i % 4, i - 6)
+        behind_head = jnp.where(split, (i - 2) % 4, jnp.where(i < 8, i % 4, (i - 6) % 4))
         head = jnp.where(lane == 0, i % 4, jnp.where(lane == 1, behind_head, (i + 3) % 4))
         return block, head
 
@@ -240,19 +242,19 @@
         def _():
             arrived(0, i)
 
-        @pl.when(i < 4)
+        @pl.when(i < jnp.where(half == 0, 2, 4))
         def _():
             send_ahead(inbox.at[0, i], i + 4)
 
-            @pl.when(half == 0)
-            def _():
-                send_across(inbox.at[0, i], i + 4)
+        @pl.when((half == 0) & (i < 4))
+        def _():
+            send_across(inbox.at[0, i], i + 4)
 
         @pl.when(i < behind_rounds)
         def _():
             arrived(1, i)
 
-        @pl.when((half == 1) & (i >= 6) & (i < 8))
+        @pl.when((i >= behind_rounds - 4) & (i < behind_rounds - 2))
         def _():
             send_behind(inbox.at[1, i], i + 2)
 
@@ -312,7 +314,7 @@
 
             lax.fori_loop(1, ring, near_start, 0)
 
-        @pl.when((i == LATE_ROUND) & (half == 0))
+        @pl.when((i == LATE_ROUND - 2) & (half == 0))
         def _():
             def forward(k, inner):
                 source = (y + k) % ring
@@ -332,12 +334,18 @@
         def _():
             run([(inbox.at[lane, i], places[lane][1], m) for lane in range(3) for m in range(members)])
 
-        @pl.when(jnp.logical_not(every))
+        last = (half == 1) & (i == ROUNDS - 1)
+
+        @pl.when(last)
+        def _():
+            run([(inbox.at[lane, i], places[lane][1], m) for lane in range(2) for m in range(members)])
+
+        @pl.when(jnp.logical_not(every | last))
         def _():
             def one(lane, inner):
                 block, g = lane_block(lane, i)
 
-                @pl.when((block < c) & ((lane < 2) | crossing))
+                @pl.when((block < c) & (i < ahead_rounds) & ((lane < 2) | crossing))
                 def _():
                     run([(inbox.at[lane, i], g, m) for m in range(members)])
 

time: 81.2 us -> 80.9 us (level)
  no operation moved by 1% of the time
where the time goes in v4:
time: 80.9 us; the launch traced here: 79.9 us
  Pallas kernels  79.3 us (98%)
    pallas_call x1, Pallas kernels, per_device(): pl.pallas_call(fused_kernel, out_shape=(jax.ShapeDtypeStruct((heads, rows...  75.9 us
    pallas_call x1, Pallas kernels, per_device(): pl.pallas_call(place_kernel, out_shape=(jax.ShapeDtypeStruct(queries.shap...  3.35 us

profile of v4, /device:TPU:28, one launch (start us, length us, event | category | flops | bytes accessed | tf_op | source)
XLA Modules:
  0.0 79.9 jit_solution(6973307763839603799)
XLA Ops:
  0.6 75.9 %shard_map.68 = (bf16[16,512,128]{2,1,0:T(8,128)(2,1)}, bf16[2,2,1,8,128,128]{5,4,3,2,1,0:T(8,128)(2,1)}) custom-call(s32[1,2]{1,0:T(1,128)} %spans_ref.1, s32[16]{0:T(128)} %partner_ref.1, bf16[512,16,128]{2,1,0:T(8,128)(2,1)} %q_ref.1, bf16[512,4,128]{2,1,0:T(4,128)(2,1)} %k_ref.1, bf16[512,4,128]{2,1,0:T(4,128)(2,1)} %v_ref.1), custom_call_target="tpu_custom_call" | custom-call | tf_op jit(solution)/shard_map/pallas_call | solution.py:437
  76.5 3.4 %shard_map.69 = (bf16[512,16,128]{2,1,0:T(8,128)(2,1)}, bf16[2,2,1,8,128,128]{5,4,3,2,1,0:T(8,128)(2,1)}) custom-call(bf16[16,512,128]{2,1,0:T(8,128)(2,1)} %get-tuple-element.4.head_ref, bf16[2,2,1,8,128,128]{5,4,3,2,1,0:T(8,128)(2,1)} %get-tuple-element.5.cache_in), custom_call_target="tpu_custom_call" | custom-call | tf_op jit(solution)/shard_map/pallas_call | solution.py:479
